TPU v7x, 32 devices: a whole 2x2x4 slice. The times are simulated.
32 devices in a mesh: scan: 2 (over y), chan: 4 (over z), tm: 2 (over x), pol: 2 (over core).
Axes of the slice: x: 2, y: 2, z: 4, core: 2. Of those that a mesh axis runs over, the one named last changes fastest.
Arguments:
- samples: int32 [2, 8, 4, 2, 16, 32768], P('pol', ('scan', 'tm'), None, None, None, 'chan'), parts along dimension 1, may hold values from 0 to 3
- pcal_phase: float32 [2, 16, 128], P('pol'), may hold values from -3.140625 to 3.140625
- tone_index: int32 [32768], P('chan'), may hold values from 0 to 127
- baseline_pairs: int32 [120, 2], replicated, may hold values from 0 to 15, as said below
Outputs:
- fringe_power: float32 [2, 8, 120, 8192], P('pol', ('scan', 'chan'), 'tm'), parts along dimension 1
There are 2 independent parts, one for each index of `scan`. A program takes and returns all parts, laid end to end along the dimension named above; an argument that names none is the same for every part. Nothing has to cross between parts.
Inputs may be any that keep to these rules, and one draw needn't show every extreme that they name: `baseline_pairs`: each row holds two different stations; every unordered pair of the 16 stations stands in exactly one row, in either order.
All inputs are finite; a program needn't handle non-finite values.
Results may differ from a plain program's by a relative error of at most 0.0029.
Values may be sent and summed in bfloat16 or wider, within the bound.
A program may use at most 256 MiB of HBM per device.

v0:
```python
import functools
import math

import jax
import jax.numpy as jnp
import numpy as np
from jax import lax
from jax.experimental import pallas as pl
from jax.experimental.pallas import tpu as pltpu
from jax.sharding import PartitionSpec as P

S = 16
NTONE = 128
ND = 8192
INNER = 256
GROUP = 3

highest = lax.Precision.HIGHEST
two_pi = 2.0 * math.pi
f32, bf16 = jnp.float32, jnp.bfloat16
MESH = pl.DeviceIdType.MESH


def split_hi_lo(value):
    high = np.asarray(value, np.float32).astype(bf16)
    low = (np.asarray(value, np.float64) - high.astype(np.float64)).astype(np.float32).astype(bf16)
    return high, low


def phase_table(left, right, modulus):
    angles = two_pi * (np.outer(left, right) % modulus) / modulus
    return np.cos(angles), np.sin(angles)


def tables(n_chan, depth):
    channels = n_chan * depth * INNER
    outer = channels // INNER
    wide = ND // outer
    outer_axis = np.arange(outer)
    inner_axis = np.arange(INNER)
    firsts = []
    for z in range(n_chan):
        fc, fs = phase_table(outer_axis, z * depth + np.arange(depth), outer)
        both = np.concatenate(
            [np.concatenate([fc, fs], axis=1), np.concatenate([-fs, fc], axis=1)], axis=0
        )
        firsts.append(np.concatenate(split_hi_lo(both), axis=1))
    twist_cos, twist_sin = phase_table(outer_axis, inner_axis, channels)
    lc, ls = phase_table(inner_axis, np.arange(wide) - wide // 2, INNER)
    last = np.concatenate(
        [np.concatenate([lc, -ls], axis=1), np.concatenate([ls, lc], axis=1)], axis=0
    )
    last = np.concatenate(split_hi_lo(last), axis=1)
    return np.stack(firsts), twist_cos.astype(np.float32), twist_sin.astype(np.float32), last


def add_scaled(total, value, factor):
    if abs(factor) < 1e-9:
        return total
    if abs(factor - 1.0) < 1e-9:
        return value if total is None else total + value
    if abs(factor + 1.0) < 1e-9:
        return -value if total is None else total - value
    return value * factor if total is None else total + value * factor


def flip_bits(z, q):
    out, bit = z, 1
    while bit <= q:
        if q & bit:
            out = out + bit * (1 - 2 * lax.rem(lax.div(z, bit), 2))
        bit *= 2
    return out


def kernel(n_tm, n_chan, group, scale, *refs):
    steps = n_chan.bit_length() - 1
    (pairs, x_ref, cos_ref, sin_ref, first_ref, tcos_ref, tsin_ref, last_ref), refs = refs[:8], refs[8:]
    out_ref, vis, outbox, twisted, spec, keep = refs[:6]
    sends, recvs = refs[6 : 6 + steps], refs[6 + steps : 6 + 2 * steps]
    tm_send, tm_recv, ch_send, ch_recv = refs[6 + 2 * steps :]

    periods, samples, _, _, depth, inner = x_ref.shape
    count = vis.shape[1]
    chunks = count // group
    rates = periods * n_tm
    outer = tcos_ref.shape[0]
    lanes = last_ref.shape[1] // 2
    me = lax.axis_index("tm")
    z = lax.axis_index("chan")

    barrier = pltpu.get_barrier_semaphore()
    for slot in range(1, n_tm):
        pl.semaphore_signal(
            barrier, inc=1, device_id={"tm": lax.rem(me + slot, n_tm)}, device_id_type=MESH
        )
    for step in range(steps):
        pl.semaphore_signal(
            barrier, inc=1, device_id={"chan": flip_bits(z, 1 << step)}, device_id_type=MESH
        )
    pl.semaphore_wait(barrier, n_tm - 1 + steps)

    def rows(chunk):
        return pl.ds(chunk * group, group)

    def tm_copy(slot, chunk):
        return pltpu.make_async_remote_copy(
            src_ref=outbox.at[slot - 1, rows(chunk)],
            dst_ref=vis.at[slot, rows(chunk)],
            send_sem=tm_send.at[slot - 1, chunk],
            recv_sem=tm_recv.at[slot - 1, chunk],
            device_id={"tm": lax.rem(me + slot, n_tm)},
            device_id_type=MESH,
        )

    def chan_copy(step, chunk):
        return pltpu.make_async_remote_copy(
            src_ref=sends[step].at[rows(chunk)],
            dst_ref=recvs[step].at[rows(chunk)],
            send_sem=ch_send.at[step, chunk],
            recv_sem=ch_recv.at[step, chunk],
            device_id={"chan": flip_bits(z, 1 << step)},
            device_id_type=MESH,
        )

    def correlate(slot, chunk):
        base = lax.rem(me + slot, n_tm) * count
        target, index = (vis, 0) if slot == 0 else (outbox, slot - 1)

        def one(k, carry):
            row = chunk * group + k
            a = pairs[base + row, 0]
            e = pairs[base + row, 1]
            ca, sa = cos_ref[a], sin_ref[a]
            ce, se = cos_ref[e], sin_ref[e]
            cos_diff = ca * ce + sa * se
            sin_diff = sa * ce - ca * se
            for period in range(periods):
                real = imag = None
                for m in range(samples):
                    ar, ai = x_ref[period, m, 0, a], x_ref[period, m, 1, a]
                    er, ei = x_ref[period, m, 0, e], x_ref[period, m, 1, e]
                    step_real = ar * er + ai * ei
                    step_imag = ai * er - ar * ei
                    real = step_real if real is None else real + step_real
                    imag = step_imag if imag is None else imag + step_imag
                real, imag = real.astype(f32), imag.astype(f32)
                both = jnp.concatenate(
                    [real * cos_diff + imag * sin_diff, imag * cos_diff - real * sin_diff], axis=0
                )
                target[index, row, period] = both.astype(bf16)
            return carry

        lax.fori_loop(0, group, one, 0)

    def outgoing(chunk):
        for slot in range(1, n_tm):
            correlate(slot, chunk)
            tm_copy(slot, chunk).start()

    def delay(chunk):
        for slot in range(1, n_tm):
            tm_copy(slot, chunk).wait_recv()

        def one(k, carry):
            row = chunk * group + k
            for slot in range(n_tm):
                for period in range(periods):
                    value = vis[slot, row, period]
                    section = jnp.dot(
                        first_ref[...],
                        jnp.concatenate([value, value], axis=0),
                        preferred_element_type=f32,
                    )
                    yr, yi = section[:outer], section[outer:]
                    tr = yr * tcos_ref[...] + yi * tsin_ref[...]
                    ti = yi * tcos_ref[...] - yr * tsin_ref[...]
                    place = slot * periods + period
                    twisted[place * outer : (place + 1) * outer, :inner] = tr.astype(bf16)
                    twisted[place * outer : (place + 1) * outer, inner:] = ti.astype(bf16)
            parts = []
            sign = jnp.where(
                lax.broadcasted_iota(jnp.int32, (outer, lanes), 1) < lanes // 2, 1.0, -1.0
            )
            for slot in range(n_tm):
                for period in range(periods):
                    place = slot * periods + period
                    both = jnp.dot(
                        twisted[place * outer : (place + 1) * outer],
                        last_ref[...],
                        preferred_element_type=f32,
                    )
                    value = both[:, :lanes] + both[:, lanes:]
                    turned = pltpu.roll(value, lanes // 2, 1) * sign
                    parts.append(((period - periods * slot) % rates, value, turned))
            for rate in range(rates):
                total = None
                for when, value, turned in parts:
                    angle = two_pi * (rate * when % rates) / rates
                    total = add_scaled(total, value, math.cos(angle))
                    total = add_scaled(total, turned, math.sin(angle))
                spec[rate] = total
            for q in range(rates):
                value = spec[flip_bits(z, q)]
                if q % 2 == 0:
                    keep[row, q // 2] = value
                else:
                    sends[0][row, q // 2] = value.astype(bf16)
            return carry

        lax.fori_loop(0, group, one, 0)
        chan_copy(0, chunk).start()

    def combine(step, chunk):
        chan_copy(step, chunk).wait_recv()

        def one(k, carry):
            row = chunk * group + k
            for j in range(recvs[step].shape[1]):
                total = keep[row, j << step] + recvs[step][row, j].astype(f32)
                if step == steps - 1:
                    turned = jnp.transpose(total)
                    half = lanes // 2
                    out_ref[row] = (turned[:half] ** 2 + turned[half:] ** 2) * scale
                elif j % 2 == 0:
                    keep[row, j << step] = total
                else:
                    sends[step + 1][row, j // 2] = total.astype(bf16)
            return carry

        lax.fori_loop(0, group, one, 0)
        if step < steps - 1:
            chan_copy(step + 1, chunk).start()

    outgoing(0)

    def round_trip(i, carry):
        @pl.when(i + 1 < chunks)
        def _():
            outgoing(i + 1)

        @pl.when(i < chunks)
        def _():
            correlate(0, i)
            delay(i)

        for step in range(steps):
            lag = step + 1

            @pl.when((i >= lag) & (i - lag < chunks))
            def _():
                combine(step, i - lag)

        return carry

    lax.fori_loop(0, chunks + steps, round_trip, 0)

    def drain(i, carry):
        for slot in range(1, n_tm):
            tm_copy(slot, i).wait_send()
        for step in range(steps):
            chan_copy(step, i).wait_send()
        return carry

    lax.fori_loop(0, chunks, drain, 0)


def fringe(n_tm, n_chan, pairs, x, cosine, sine, first, twist_cos, twist_sin, last):
    steps = n_chan.bit_length() - 1
    periods, samples, _, _, depth, inner = x.shape
    rates = periods * n_tm
    count = pairs.shape[0] // n_tm
    group = max(g for g in range(1, GROUP + 1) if count % g == 0)
    chunks = count // group
    outer = twist_cos.shape[0]
    lanes = last.shape[1] // 2
    channels = n_chan * depth * inner
    scale = 1.0 / (100.0 * samples * rates * channels)
    tile = (outer, lanes)
    boxes = [pltpu.VMEM((count, rates >> (s + 1)) + tile, bf16) for s in range(steps)]
    vmem = pl.BlockSpec(memory_space=pltpu.VMEM)
    return pl.pallas_call(
        functools.partial(kernel, n_tm, n_chan, group, scale),
        out_shape=jax.ShapeDtypeStruct((count, lanes // 2, outer), f32),
        in_specs=[pl.BlockSpec(memory_space=pltpu.SMEM)] + [vmem] * 7,
        out_specs=vmem,
        scratch_shapes=[
            pltpu.VMEM((n_tm, count, periods, 2 * depth, inner), bf16),
            pltpu.VMEM((n_tm - 1, count, periods, 2 * depth, inner), bf16),
            pltpu.VMEM((rates * outer, 2 * inner), bf16),
            pltpu.VMEM((rates,) + tile, f32),
            pltpu.VMEM((count, rates // 2) + tile, f32),
        ]
        + boxes
        + boxes
        + [
            pltpu.SemaphoreType.DMA((n_tm - 1, chunks)),
            pltpu.SemaphoreType.DMA((n_tm - 1, chunks)),
            pltpu.SemaphoreType.DMA((steps, chunks)),
            pltpu.SemaphoreType.DMA((steps, chunks)),
        ],
        compiler_params=pltpu.CompilerParams(
            collective_id=0, has_side_effects=True, vmem_limit_bytes=60 << 20
        ),
        name="fringe",
    )(pairs, x, cosine, sine, first, twist_cos, twist_sin, last)


def shards(samples, pcal_phase, tone_index, baseline_pairs):
    n_tm = lax.axis_size("tm")
    n_chan = lax.axis_size("chan")
    z = lax.axis_index("chan")
    _, nt_dev, m, _, _, width = samples.shape
    depth = width // INNER

    x = (2 * samples[0] - 3).astype(bf16).reshape(nt_dev, m, 2, S, depth, INNER)
    tone_slots = (tone_index[None, :] == jnp.arange(NTONE, dtype=jnp.int32)[:, None]).astype(f32)
    cosine = jnp.dot(jnp.cos(pcal_phase[0]), tone_slots, precision=highest).reshape(S, depth, INNER)
    sine = jnp.dot(jnp.sin(pcal_phase[0]), tone_slots, precision=highest).reshape(S, depth, INNER)

    firsts, twist_cos, twist_sin, last = tables(n_chan, depth)
    first = lax.dynamic_index_in_dim(jnp.asarray(firsts), z, 0, keepdims=False)
    power = fringe(
        n_tm, n_chan, baseline_pairs, x, cosine, sine, first,
        jnp.asarray(twist_cos), jnp.asarray(twist_sin), jnp.asarray(last),
    )
    return power.reshape(1, 1, power.shape[0], ND)


def solution(mesh):
    placed = (
        P("pol", ("scan", "tm"), None, None, None, "chan"),
        P("pol", None, None),
        P("chan"),
        P(),
    )
    return jax.shard_map(
        shards,
        mesh=mesh,
        in_specs=placed,
        out_specs=P("pol", ("scan", "chan"), "tm", None),
        check_vma=False,
    )
```

profile of v0, /device:TPU:0, one launch (start us, length us, event | category | flops | bytes accessed | tf_op | source)
XLA Modules:
  0.0 165.9 jit_solution(12106742231057711470)
XLA Ops:
  0.0 1.4 copy.11.refs_0_
  1.4 4.4 %add_convert_fusion = bf16[1,2,4,2,16,8192]{5,4,3,2,1,0:T(8,128)(2,1)S(1)} fusion(s32[1,2,4,2,16,8192]{5,4,3,2,1,0:T(8,128)} %param.8), kind=kLoop, calls=%fused_computation | loop fusion | flops 6291456 | bytes 12582912 | tf_op jit(solution)/shard_map/convert_element_type | solution.py:316
  5.9 0.0 copy-start
  5.9 0.0 copy-start.1
  5.9 3.3 %copy.13 = bf16[32,8,32,256]{3,2,1,0:T(8,128)(2,1)} copy(bf16[32,8,32,256]{3,1,2,0:T(8,128)(2,1)S(1)} %bitcast.20) | data formatting | bytes 8388608
  9.2 0.0 copy-done
  9.2 0.0 copy-done.1
  9.2 1.4 fusion.1
  10.6 1.0 copy.14
  11.6 1.4 fusion
  13.0 1.0 copy.15
  13.9 1.5 dynamic-slice_bitcast_fusion.refs_4_
  15.4 147.4 %fringe.1 = f32[60,64,128]{2,1,0:T(8,128)} custom-call(s32[120,2]{1,0:T(8,128)} %copy.11.refs_0_, bf16[2,4,2,16,32,256]{5,4,3,2,1,0:T(8,128)(2,1)} %bitcast.21, f32[16,32,256]{2,1,0:T(8,128)} %bitcast.23, f32[16,32,256]{2,1,0:T(8,128)} %bitcast.24, bf16[256,128]{1,0:T(8,128)(2,1)} %dynamic-slice_bitcast_fusion.refs_4_, f32[128,256]{1,0:T(8,128)} %constant.25.clone.refs_5_, ...), custom_call_target="tpu_custom_call" | custom-call | tf_op jit(solution)/shard_map/fringe/pallas_call | solution.py:282
  162.8 3.0 %copy.17 = f32[1,1,60,8192]{3,1,2,0:T(1,128)} copy(f32[1,1,60,8192]{3,1,2,0:T(1,128)} %bitcast.22) | data formatting | bytes 3932160
Async XLA Ops:
  5.9 3.3 %copy-start = (s32[8192]{0:T(1024)S(1)}, s32[8192]{0:T(1024)}, u32[]{:S(2)}) copy-start(s32[8192]{0:T(1024)} %param.10) | copy-start | bytes 98308
  5.9 3.3 %copy-start.1 = (f32[1,16,128]{2,1,0:T(8,128)S(1)}, f32[1,16,128]{2,1,0:T(8,128)}, u32[]{:S(2)}) copy-start(f32[1,16,128]{2,1,0:T(8,128)} %param.9) | copy-start | bytes 24580
where the time goes:
time: 166 us
  Pallas kernels  147 us (89%)
  local copies, waits for them, and re-layouts  11.2 us (7%)
  other arithmetic  4.44 us (3%)
  matrix products  2.83 us (2%)
    pallas_call x1, Pallas kernels, fringe(): pl.pallas_call(functools.partial(kernel, n_tm, n_chan, group, scale), out...  147 us
    unnamed x9, local copies, waits for them, and re-layouts  9.69 us
    convert_element_type x1, other arithmetic, shards(): x = (2 * samples[0] - 3).astype(bf16).reshape(nt_dev, m, 2, S, depth, INNER)  4.44 us

commit v1 on v0

--- a/solution.py
+++ b/solution.py
@@ -10,12 +10,14 @@
 from jax.sharding import PartitionSpec as P
 
 S = 16
-NTONE = 128
 ND = 8192
+LANES = 128
+SUB = 8
 INNER = 256
-GROUP = 3
-
-highest = lax.Precision.HIGHEST
+GROUP = 1
+AHEAD = 2
+LAG = 3
+
 two_pi = 2.0 * math.pi
 f32, bf16 = jnp.float32, jnp.bfloat16
 MESH = pl.DeviceIdType.MESH
@@ -75,19 +77,41 @@
 
 def kernel(n_tm, n_chan, group, scale, *refs):
     steps = n_chan.bit_length() - 1
-    (pairs, x_ref, cos_ref, sin_ref, first_ref, tcos_ref, tsin_ref, last_ref), refs = refs[:8], refs[8:]
-    out_ref, vis, outbox, twisted, spec, keep = refs[:6]
-    sends, recvs = refs[6 : 6 + steps], refs[6 + steps : 6 + 2 * steps]
-    tm_send, tm_recv, ch_send, ch_recv = refs[6 + 2 * steps :]
-
-    periods, samples, _, _, depth, inner = x_ref.shape
+    (pairs, samples_ref, tones_in, pcal_in, firsts, *tables_in), refs = refs[:8], refs[8:]
+    (out_ref, codes, x_ref, tones, pcal, cos_ref, sin_ref), refs = refs[:7], refs[7:]
+    (first_ref, tcos_ref, tsin_ref, last_ref), refs = refs[:4], refs[4:]
+    (vis, outbox, twisted, spec, keep), refs = refs[:5], refs[5:]
+    sends, recvs = refs[:steps], refs[steps : 2 * steps]
+    phase_sem, code_sem, table_sem, tm_send, tm_recv, ch_send, ch_recv = refs[2 * steps :]
+
+    periods, samples, _, stations, depth, inner = x_ref.shape
     count = vis.shape[1]
     chunks = count // group
     rates = periods * n_tm
     outer = tcos_ref.shape[0]
     lanes = last_ref.shape[1] // 2
+    halves = inner // LANES
     me = lax.axis_index("tm")
     z = lax.axis_index("chan")
+
+    phases = [
+        pltpu.make_async_copy(tones_in, tones, phase_sem.at[0]),
+        pltpu.make_async_copy(pcal_in.at[0], pcal, phase_sem.at[1]),
+    ]
+    fetches = [
+        pltpu.make_async_copy(samples_ref.at[period], codes.at[period], code_sem.at[period])
+        for period in range(periods)
+    ]
+    for copy in phases + fetches:
+        copy.start()
+    constants = [
+        pltpu.make_async_copy(source, target, table_sem.at[i])
+        for i, (source, target) in enumerate(
+            zip([firsts.at[z]] + tables_in, [first_ref, tcos_ref, tsin_ref, last_ref])
+        )
+    ]
+    for copy in constants:
+        copy.start()
 
     barrier = pltpu.get_barrier_semaphore()
     for slot in range(1, n_tm):
@@ -98,26 +122,69 @@
         pl.semaphore_signal(
             barrier, inc=1, device_id={"chan": flip_bits(z, 1 << step)}, device_id_type=MESH
         )
+
+    def station_table(station, carry):
+        phase = pcal[pl.ds(station, 1), :]
+        for turn, target in ((jnp.cos, cos_ref), (jnp.sin, sin_ref)):
+            row = jnp.broadcast_to(turn(phase), (depth, LANES))
+            for half in range(halves):
+                index = tones[pl.ds(half, depth, stride=halves), :]
+                target[station, :, half * LANES : (half + 1) * LANES] = jnp.take_along_axis(
+                    row, index, axis=1
+                )
+        return carry
+
+    for copy in phases:
+        copy.wait()
+    lax.fori_loop(0, stations, station_table, 0)
+
+    for period in range(periods):
+        fetches[period].wait()
+
+        def levels(station, carry):
+            for m in range(samples):
+                for part in range(2):
+                    for half in range(halves):
+                        start = lax.div(station, SUB) * (depth * halves * SUB) + half * SUB
+                        code = codes[
+                            period,
+                            m,
+                            part,
+                            pl.ds(start + lax.rem(station, SUB), depth, stride=halves * SUB),
+                            :,
+                        ]
+                        x_ref[
+                            period, m, part, station, :, half * LANES : (half + 1) * LANES
+                        ] = (2 * code - 3).astype(f32).astype(bf16)
+            return carry
+
+        lax.fori_loop(0, stations, levels, 0)
+    for copy in constants:
+        copy.wait()
     pl.semaphore_wait(barrier, n_tm - 1 + steps)
 
     def rows(chunk):
         return pl.ds(chunk * group, group)
 
-    def tm_copy(slot, chunk):
+    everything = pl.ds(0, count)
+
+    def tm_copy(slot, chunk, block=None):
+        block = rows(chunk) if block is None else block
         return pltpu.make_async_remote_copy(
-            src_ref=outbox.at[slot - 1, rows(chunk)],
-            dst_ref=vis.at[slot, rows(chunk)],
-            send_sem=tm_send.at[slot - 1, chunk],
+            src_ref=outbox.at[slot - 1, block],
+            dst_ref=vis.at[slot, block],
+            send_sem=tm_send.at[slot - 1],
             recv_sem=tm_recv.at[slot - 1, chunk],
             device_id={"tm": lax.rem(me + slot, n_tm)},
             device_id_type=MESH,
         )
 
-    def chan_copy(step, chunk):
+    def chan_copy(step, chunk, block=None):
+        block = rows(chunk) if block is None else block
         return pltpu.make_async_remote_copy(
-            src_ref=sends[step].at[rows(chunk)],
-            dst_ref=recvs[step].at[rows(chunk)],
-            send_sem=ch_send.at[step, chunk],
+            src_ref=sends[step].at[block],
+            dst_ref=recvs[step].at[block],
+            send_sem=ch_send.at[step],
             recv_sem=ch_recv.at[step, chunk],
             device_id={"chan": flip_bits(z, 1 << step)},
             device_id_type=MESH,
@@ -129,8 +196,8 @@
 
         def one(k, carry):
             row = chunk * group + k
-            a = pairs[base + row, 0]
-            e = pairs[base + row, 1]
+            a = pairs[0, base + row]
+            e = pairs[1, base + row]
             ca, sa = cos_ref[a], sin_ref[a]
             ce, se = cos_ref[e], sin_ref[e]
             cos_diff = ca * ce + sa * se
@@ -232,12 +299,13 @@
         if step < steps - 1:
             chan_copy(step + 1, chunk).start()
 
-    outgoing(0)
+    for i in range(min(AHEAD, chunks)):
+        outgoing(i)
 
     def round_trip(i, carry):
-        @pl.when(i + 1 < chunks)
+        @pl.when(i + AHEAD < chunks)
         def _():
-            outgoing(i + 1)
+            outgoing(i + AHEAD)
 
         @pl.when(i < chunks)
         def _():
@@ -245,7 +313,7 @@
             delay(i)
 
         for step in range(steps):
-            lag = step + 1
+            lag = LAG * (step + 1)
 
             @pl.when((i >= lag) & (i - lag < chunks))
             def _():
@@ -253,76 +321,81 @@
 
         return carry
 
-    lax.fori_loop(0, chunks + steps, round_trip, 0)
-
-    def drain(i, carry):
-        for slot in range(1, n_tm):
-            tm_copy(slot, i).wait_send()
-        for step in range(steps):
-            chan_copy(step, i).wait_send()
-        return carry
-
-    lax.fori_loop(0, chunks, drain, 0)
-
-
-def fringe(n_tm, n_chan, pairs, x, cosine, sine, first, twist_cos, twist_sin, last):
+    lax.fori_loop(0, chunks + steps * LAG, round_trip, 0)
+
+    for slot in range(1, n_tm):
+        tm_copy(slot, 0, everything).wait_send()
+    for step in range(steps):
+        chan_copy(step, 0, everything).wait_send()
+
+
+def fringe(n_tm, n_chan, pairs, tones, pcal_phase, samples):
     steps = n_chan.bit_length() - 1
-    periods, samples, _, _, depth, inner = x.shape
+    _, periods, taken, _, stations, width = samples.shape
+    depth = width // INNER
+    rowed = samples.reshape(periods, taken, 2, stations // SUB, SUB, width // LANES, LANES)
+    rowed = rowed.transpose(0, 1, 2, 3, 5, 4, 6).reshape(periods, taken, 2, -1, LANES)
     rates = periods * n_tm
-    count = pairs.shape[0] // n_tm
+    count = pairs.shape[1] // n_tm
     group = max(g for g in range(1, GROUP + 1) if count % g == 0)
     chunks = count // group
+    constants = tables(n_chan, depth)
+    firsts, twist_cos, _, last = constants
     outer = twist_cos.shape[0]
     lanes = last.shape[1] // 2
-    channels = n_chan * depth * inner
-    scale = 1.0 / (100.0 * samples * rates * channels)
+    scale = 1.0 / (100.0 * taken * rates * n_chan * width)
     tile = (outer, lanes)
     boxes = [pltpu.VMEM((count, rates >> (s + 1)) + tile, bf16) for s in range(steps)]
     vmem = pl.BlockSpec(memory_space=pltpu.VMEM)
+    stay = pl.BlockSpec(memory_space=pltpu.HBM)
     return pl.pallas_call(
         functools.partial(kernel, n_tm, n_chan, group, scale),
-        out_shape=jax.ShapeDtypeStruct((count, lanes // 2, outer), f32),
-        in_specs=[pl.BlockSpec(memory_space=pltpu.SMEM)] + [vmem] * 7,
+        out_shape=pltpu.VMEM((count, lanes // 2, outer), f32),
+        in_specs=[pl.BlockSpec(memory_space=pltpu.SMEM)] + [stay] * 7,
         out_specs=vmem,
         scratch_shapes=[
-            pltpu.VMEM((n_tm, count, periods, 2 * depth, inner), bf16),
-            pltpu.VMEM((n_tm - 1, count, periods, 2 * depth, inner), bf16),
-            pltpu.VMEM((rates * outer, 2 * inner), bf16),
+            pltpu.VMEM((periods, taken, 2, width // LANES * stations, LANES), jnp.int32),
+            pltpu.VMEM((periods, taken, 2, stations, depth, INNER), bf16),
+            pltpu.VMEM(tones.shape, jnp.int32),
+            pltpu.VMEM(pcal_phase.shape[1:], f32),
+            pltpu.VMEM((stations, depth, INNER), f32),
+            pltpu.VMEM((stations, depth, INNER), f32),
+            pltpu.VMEM(firsts.shape[1:], bf16),
+            pltpu.VMEM(twist_cos.shape, f32),
+            pltpu.VMEM(twist_cos.shape, f32),
+            pltpu.VMEM(last.shape, bf16),
+            pltpu.VMEM((n_tm, count, periods, 2 * depth, INNER), bf16),
+            pltpu.VMEM((n_tm - 1, count, periods, 2 * depth, INNER), bf16),
+            pltpu.VMEM((rates * outer, 2 * INNER), bf16),
             pltpu.VMEM((rates,) + tile, f32),
             pltpu.VMEM((count, rates // 2) + tile, f32),
         ]
         + boxes
         + boxes
         + [
+            pltpu.SemaphoreType.DMA((2,)),
+            pltpu.SemaphoreType.DMA((periods,)),
+            pltpu.SemaphoreType.DMA((len(constants),)),
+            pltpu.SemaphoreType.DMA((n_tm - 1,)),
             pltpu.SemaphoreType.DMA((n_tm - 1, chunks)),
-            pltpu.SemaphoreType.DMA((n_tm - 1, chunks)),
-            pltpu.SemaphoreType.DMA((steps, chunks)),
+            pltpu.SemaphoreType.DMA((steps,)),
             pltpu.SemaphoreType.DMA((steps, chunks)),
         ],
         compiler_params=pltpu.CompilerParams(
-            collective_id=0, has_side_effects=True, vmem_limit_bytes=60 << 20
+            collective_id=0, has_side_effects=True, vmem_limit_bytes=57 << 20
         ),
         name="fringe",
-    )(pairs, x, cosine, sine, first, twist_cos, twist_sin, last)
+    )(pairs, rowed, tones, pcal_phase, *(jnp.asarray(c) for c in constants))
 
 
 def shards(samples, pcal_phase, tone_index, baseline_pairs):
-    n_tm = lax.axis_size("tm")
-    n_chan = lax.axis_size("chan")
-    z = lax.axis_index("chan")
-    _, nt_dev, m, _, _, width = samples.shape
-    depth = width // INNER
-
-    x = (2 * samples[0] - 3).astype(bf16).reshape(nt_dev, m, 2, S, depth, INNER)
-    tone_slots = (tone_index[None, :] == jnp.arange(NTONE, dtype=jnp.int32)[:, None]).astype(f32)
-    cosine = jnp.dot(jnp.cos(pcal_phase[0]), tone_slots, precision=highest).reshape(S, depth, INNER)
-    sine = jnp.dot(jnp.sin(pcal_phase[0]), tone_slots, precision=highest).reshape(S, depth, INNER)
-
-    firsts, twist_cos, twist_sin, last = tables(n_chan, depth)
-    first = lax.dynamic_index_in_dim(jnp.asarray(firsts), z, 0, keepdims=False)
     power = fringe(
-        n_tm, n_chan, baseline_pairs, x, cosine, sine, first,
-        jnp.asarray(twist_cos), jnp.asarray(twist_sin), jnp.asarray(last),
+        lax.axis_size("tm"),
+        lax.axis_size("chan"),
+        baseline_pairs.T,
+        tone_index.reshape(-1, LANES),
+        pcal_phase,
+        samples,
     )
     return power.reshape(1, 1, power.shape[0], ND)
 

time: 166 us -> 150 us (0.904)
  local copies, waits for them, and re-layouts: 11.2 us -> 1.27 us
  other arithmetic: 4.44 us -> 0 us
  matrix products: 2.83 us -> 0 us
    unnamed x9 -> x1, local copies, waits for them, and re-layouts: 9.69 us -> 1.27 us
    convert_element_type x1 -> x0, other arithmetic: 4.44 us -> none  [shards(): x = (2 * samples[0] - 3).astype(bf16).reshape(nt_dev, m, 2, S, depth, INNER)]
    dot_general x2 -> x0, matrix products: 2.83 us -> none  [the longest x1 1.42 us: shards(): jnp.dot(jnp.sin(pcal_phase[0]), tone_slots, precision=highest)]
where the time goes in v1:
time: 150 us
  Pallas kernels  148 us (99%)
    pallas_call x1, Pallas kernels, fringe(): pl.pallas_call(functools.partial(kernel, n_tm, n_chan, group, scale), out...  148 us

profile of v1, /device:TPU:0, one launch (start us, length us, event | category | flops | bytes accessed | tf_op | source)
XLA Modules:
  0.0 149.6 jit_solution(2653360758284983221)
XLA Ops:
  0.0 148.3 %fringe.1 = f32[60,64,128]{2,1,0:T(8,128)S(1)} custom-call(s32[2,120]{1,0:T(2,128)} %bitcast.11, s32[2,4,2,1024,128]{4,3,2,1,0:T(8,128)} %bitcast.9, s32[64,128]{1,0:T(8,128)} %bitcast.10, f32[1,16,128]{2,1,0:T(8,128)} %refs_3_.1, bf16[4,256,128]{2,1,0:T(8,128)(2,1)} %constant.8.clone.refs_4_, f32[128,256]{1,0:T(8,128)} %constant.9.clone.refs_5_, ...), custom_call_target="tpu_custom_call" | custom-call | tf_op jit(solution)/shard_map/fringe/pallas_call | solution.py:351
  148.3 1.3 copy.12

commit v2 on v1

--- a/solution.py
+++ b/solution.py
@@ -17,6 +17,9 @@
 GROUP = 1
 AHEAD = 2
 LAG = 3
+LENT = 8
+FAR_AHEAD = 16
+LENT_AHEAD = 10
 
 two_pi = 2.0 * math.pi
 f32, bf16 = jnp.float32, jnp.bfloat16
@@ -388,10 +391,491 @@
     )(pairs, rowed, tones, pcal_phase, *(jnp.asarray(c) for c in constants))
 
 
+def lending_tables(n_chan, depth, lent):
+    firsts, twist_cos, twist_sin, last = tables(n_chan, depth)
+    width = 2 * depth
+    rows = np.concatenate([np.arange(lent), depth + np.arange(lent)])
+    rest = np.concatenate([np.arange(lent, depth), depth + np.arange(lent, depth)])
+    own, added = [], []
+    for z in range(n_chan):
+        high, low = firsts[z][:, :width], firsts[z][:, width:]
+        own.append(np.concatenate([high, high, low], axis=1))
+        high, low = firsts[z ^ 1][:, :width], firsts[z ^ 1][:, width:]
+        added.append(
+            np.concatenate(
+                [high[:, rows], high[:, rows], low[:, rows], high[:, rest], low[:, rest]], axis=1
+            )
+        )
+    both = np.concatenate([np.stack(own), np.stack(added)], axis=2)
+    return both, twist_cos, twist_sin, last
+
+
+def lending_kernel(n_tm, scale, names, *flat):
+    ref = dict(zip(names, flat))
+    out_ref, codes, x_ref, lent_x = ref["out"], ref["codes"], ref["x"], ref["lent_x"]
+    vis, outbox, lent_vis, lent_box = ref["vis"], ref["outbox"], ref["lent_vis"], ref["lent_box"]
+    waves, lent_waves, passed = ref["waves"], ref["lent_waves"], ref["passed"]
+    twisted, keep, cross_out, cross_in = ref["twisted"], ref["keep"], ref["cross_out"], ref["cross_in"]
+    first_ref, tcos_ref, tsin_ref, last_ref = ref["first"], ref["tcos"], ref["tsin"], ref["last"]
+    pairs, tones = ref["pairs"], ref["tones"]
+
+    periods, samples, _, stations, depth, inner = x_ref.shape
+    lent = lent_x.shape[4]
+    count = vis.shape[1]
+    rates = periods * n_tm
+    outer = tcos_ref.shape[0]
+    lanes = last_ref.shape[1] // 2
+    halves = inner // LANES
+    own_width = 6 * depth
+    me = lax.axis_index("tm")
+    z = lax.axis_index("chan")
+    buddy = flip_bits(z, 1)
+    across = flip_bits(z, 3)
+    is_end = lax.rem(z, 3) == 0
+    is_inner = lax.rem(z, 3) != 0
+
+    def start_all(copies):
+        for copy in copies:
+            copy.start()
+
+    def wait_all(copies):
+        for copy in copies:
+            copy.wait()
+
+    phases = [
+        pltpu.make_async_copy(ref["tones_in"], tones, ref["phase_sem"].at[0]),
+        pltpu.make_async_copy(ref["pcal_in"].at[0], ref["pcal"], ref["phase_sem"].at[1]),
+    ]
+    fetches = [
+        pltpu.make_async_copy(ref["samples"].at[p], codes.at[p], ref["code_sem"].at[p])
+        for p in range(periods)
+    ]
+    constants = [
+        pltpu.make_async_copy(source, target, ref["table_sem"].at[i])
+        for i, (source, target) in enumerate(
+            [
+                (ref["firsts"].at[z], first_ref),
+                (ref["tcos_in"], tcos_ref),
+                (ref["tsin_in"], tsin_ref),
+                (ref["last_in"], last_ref),
+            ]
+        )
+    ]
+    start_all(phases + fetches + constants)
+
+    barrier = pltpu.get_barrier_semaphore()
+    for slot in range(1, n_tm):
+        pl.semaphore_signal(
+            barrier, inc=1, device_id={"tm": lax.rem(me + slot, n_tm)}, device_id_type=MESH
+        )
+    pl.semaphore_signal(barrier, inc=1, device_id={"chan": buddy}, device_id_type=MESH)
+
+    @pl.when(is_inner)
+    def _():
+        pl.semaphore_signal(barrier, inc=1, device_id={"chan": across}, device_id_type=MESH)
+
+    def station_tables(source, cos_ref, sin_ref):
+        tall = cos_ref.shape[1]
+
+        def one(station, carry):
+            phase = ref["pcal"][pl.ds(station, 1), :]
+            for turn, target in ((jnp.cos, cos_ref), (jnp.sin, sin_ref)):
+                row = jnp.broadcast_to(turn(phase), (tall, LANES))
+                for half in range(halves):
+                    index = source[pl.ds(half, tall, stride=halves), :]
+                    target[station, :, half * LANES : (half + 1) * LANES] = jnp.take_along_axis(
+                        row, index, axis=1
+                    )
+            return carry
+
+        lax.fori_loop(0, stations, one, 0)
+
+    def lend(period):
+        return pltpu.make_async_remote_copy(
+            src_ref=x_ref.at[period, :, :, :, pl.ds(0, lent)],
+            dst_ref=lent_x.at[period],
+            send_sem=ref["lend_send"].at[period],
+            recv_sem=ref["lend_recv"].at[period],
+            device_id={"chan": buddy},
+            device_id_type=MESH,
+        )
+
+    lend_tones = pltpu.make_async_remote_copy(
+        src_ref=tones,
+        dst_ref=ref["lent_tones"],
+        send_sem=ref["lend_send"].at[periods],
+        recv_sem=ref["lend_recv"].at[periods],
+        device_id={"chan": buddy},
+        device_id_type=MESH,
+    )
+
+    wait_all(phases)
+    station_tables(tones, ref["cos"], ref["sin"])
+    for period in range(periods):
+        fetches[period].wait()
+
+        def levels(station, carry):
+            for m in range(samples):
+                for part in range(2):
+                    for half in range(halves):
+                        start = lax.div(station, SUB) * (depth * halves * SUB) + half * SUB
+                        code = codes[
+                            period,
+                            m,
+                            part,
+                            pl.ds(start + lax.rem(station, SUB), depth, stride=halves * SUB),
+                            :,
+                        ]
+                        x_ref[
+                            period, m, part, station, :, half * LANES : (half + 1) * LANES
+                        ] = (2 * code - 3).astype(f32).astype(bf16)
+            return carry
+
+        lax.fori_loop(0, stations, levels, 0)
+        if period == 0:
+
+            @pl.when(is_end)
+            def _():
+                pl.semaphore_wait(barrier, n_tm)
+
+            @pl.when(is_inner)
+            def _():
+                pl.semaphore_wait(barrier, n_tm + 1)
+
+        @pl.when(is_end)
+        def _():
+            lend(period).start()
+
+    @pl.when(is_end)
+    def _():
+        lend_tones.start()
+
+    wait_all(constants)
+
+    def tm_copy(slot, row, size=1):
+        block = pl.ds(row, size)
+        return pltpu.make_async_remote_copy(
+            src_ref=outbox.at[slot - 1, block],
+            dst_ref=vis.at[slot, block],
+            send_sem=ref["tm_send"].at[slot - 1],
+            recv_sem=ref["tm_recv"].at[slot - 1, row],
+            device_id={"tm": lax.rem(me + slot, n_tm)},
+            device_id_type=MESH,
+        )
+
+    def lent_copy(slot, row, size=1):
+        block = pl.ds(row, size)
+        return pltpu.make_async_remote_copy(
+            src_ref=lent_box.at[slot - 1, block],
+            dst_ref=lent_vis.at[slot, block],
+            send_sem=ref["tm_lent_send"].at[slot - 1],
+            recv_sem=ref["tm_lent_recv"].at[slot - 1, row],
+            device_id={"tm": lax.rem(me + slot, n_tm)},
+            device_id_type=MESH,
+        )
+
+    def pass_copy(row, size=1):
+        block = pl.ds(row, size)
+        return pltpu.make_async_remote_copy(
+            src_ref=passed.at[block],
+            dst_ref=passed.at[block],
+            send_sem=ref["pass_send"],
+            recv_sem=ref["pass_recv"].at[row],
+            device_id={"chan": buddy},
+            device_id_type=MESH,
+        )
+
+    def cross_copy(row, size=1):
+        block = pl.ds(row, size)
+        return pltpu.make_async_remote_copy(
+            src_ref=cross_out.at[block],
+            dst_ref=cross_in.at[block],
+            send_sem=ref["cross_send"],
+            recv_sem=ref["sum_recv"].at[row],
+            device_id={"chan": across},
+            device_id_type=MESH,
+        )
+
+    def back_copy(row, size=1):
+        block = pl.ds(row, size)
+        return pltpu.make_async_remote_copy(
+            src_ref=keep.at[1, block],
+            dst_ref=keep.at[1, block],
+            send_sem=ref["back_send"],
+            recv_sem=ref["sum_recv"].at[row],
+            device_id={"chan": buddy},
+            device_id_type=MESH,
+        )
+
+    def correlate(slot, row, voltage, cos_ref, sin_ref, target, index):
+        place = lax.rem(me + slot, n_tm) * count + row
+        a = pairs[0, place]
+        e = pairs[1, place]
+        ca, sa = cos_ref[a], sin_ref[a]
+        ce, se = cos_ref[e], sin_ref[e]
+        cos_diff = ca * ce + sa * se
+        sin_diff = sa * ce - ca * se
+        for period in range(periods):
+            real = imag = None
+            for m in range(samples):
+                ar, ai = voltage[period, m, 0, a], voltage[period, m, 1, a]
+                er, ei = voltage[period, m, 0, e], voltage[period, m, 1, e]
+                step_real = ar * er + ai * ei
+                step_imag = ai * er - ar * ei
+                real = step_real if real is None else real + step_real
+                imag = step_imag if imag is None else imag + step_imag
+            real, imag = real.astype(f32), imag.astype(f32)
+            both = jnp.concatenate(
+                [real * cos_diff + imag * sin_diff, imag * cos_diff - real * sin_diff], axis=0
+            )
+            target[index, row, period] = both.astype(bf16)
+
+    def own_visibility(slot, row):
+        target, index = (vis, 0) if slot == 0 else (outbox, slot - 1)
+        correlate(slot, row, x_ref, ref["cos"], ref["sin"], target, index)
+
+    def lent_visibility(slot, row):
+        target, index = (lent_vis, 0) if slot == 0 else (lent_box, slot - 1)
+        correlate(slot, row, lent_x, ref["lent_cos"], ref["lent_sin"], target, index)
+
+    def outgoing(row):
+        for slot in range(1, n_tm):
+            own_visibility(slot, row)
+            tm_copy(slot, row).start()
+
+    def lent_outgoing(row):
+        for slot in range(1, n_tm):
+            lent_visibility(slot, row)
+            lent_copy(slot, row).start()
+
+    def spectra(source, row, target):
+        tall = target.shape[1] // 2
+        parts = []
+        for slot in range(n_tm):
+            for period in range(periods):
+                value = source[slot, row, period].astype(f32)
+                parts.append(((period - periods * slot) % rates, value[:tall], value[tall:]))
+        for rate in range(rates):
+            real = imag = None
+            for when, vr, vi in parts:
+                angle = two_pi * (rate * when % rates) / rates
+                c, s = math.cos(angle), math.sin(angle)
+                real = add_scaled(add_scaled(real, vr, c), vi, s)
+                imag = add_scaled(add_scaled(imag, vi, c), vr, -s)
+            target[rate, :tall] = real
+            target[rate, tall:] = imag
+
+    def halves_of(value):
+        high = value.astype(bf16)
+        low = (value - high.astype(f32)).astype(bf16)
+        return [high, low, high]
+
+    def stage_one(place, columns, blocks):
+        section = jnp.dot(
+            columns, jnp.concatenate(blocks, axis=0), preferred_element_type=f32
+        )
+        yr, yi = section[:outer], section[outer:]
+        tr = yr * tcos_ref[...] + yi * tsin_ref[...]
+        ti = yi * tcos_ref[...] - yr * tsin_ref[...]
+        twisted[place * outer : (place + 1) * outer, :inner] = tr.astype(bf16)
+        twisted[place * outer : (place + 1) * outer, inner:] = ti.astype(bf16)
+
+    def stage_two(place):
+        both = jnp.dot(
+            twisted[place * outer : (place + 1) * outer],
+            last_ref[...],
+            preferred_element_type=f32,
+        )
+        return both[:, :lanes] + both[:, lanes:]
+
+    def finish(row, total):
+        turned = jnp.transpose(total)
+        half = lanes // 2
+        out_ref[row] = (turned[:half] ** 2 + turned[half:] ** 2) * scale
+
+    @pl.when(is_end)
+    def _():
+        def send_rows(row, carry):
+            outgoing(row)
+            return carry
+
+        lax.fori_loop(0, count, send_rows, 0)
+        for period in range(periods):
+            lend(period).wait_send()
+        lend_tones.wait_send()
+
+        def one(row, carry):
+            own_visibility(0, row)
+            for slot in range(1, n_tm):
+                tm_copy(slot, row).wait_recv()
+            spectra(vis, row, waves)
+            for q in range(1, rates):
+                value = waves[flip_bits(z, q)]
+                rest = jnp.concatenate([value[lent:depth], value[depth + lent :]], axis=0)
+                passed[row, q - 1] = rest.astype(bf16)
+            pass_copy(row).start()
+            stage_one(0, first_ref[:, :own_width], halves_of(waves[z]))
+            keep[0, row] = stage_two(0)
+            return carry
+
+        lax.fori_loop(0, count, one, 0)
+
+        def close(row, carry):
+            back_copy(row).wait_recv()
+            finish(row, keep[0, row] + keep[1, row])
+            return carry
+
+        lax.fori_loop(0, count, close, 0)
+        pass_copy(0, count).wait_send()
+
+    @pl.when(is_inner)
+    def _():
+        def send_rows(row, carry):
+            outgoing(row)
+            return carry
+
+        lax.fori_loop(0, min(FAR_AHEAD, count), send_rows, 0)
+        for period in range(periods):
+            lend(period).wait_recv()
+        lend_tones.wait_recv()
+        station_tables(ref["lent_tones"], ref["lent_cos"], ref["lent_sin"])
+
+        def lend_rows(row, carry):
+            lent_outgoing(row)
+            return carry
+
+        lax.fori_loop(0, min(LENT_AHEAD, count), lend_rows, 0)
+
+        def one(row, carry):
+            @pl.when(row + FAR_AHEAD < count)
+            def _():
+                outgoing(row + FAR_AHEAD)
+
+            @pl.when(row + LENT_AHEAD < count)
+            def _():
+                lent_outgoing(row + LENT_AHEAD)
+
+            @pl.when(row < count)
+            def _():
+                own_visibility(0, row)
+                lent_visibility(0, row)
+                for slot in range(1, n_tm):
+                    tm_copy(slot, row).wait_recv()
+                    lent_copy(slot, row).wait_recv()
+                spectra(vis, row, waves)
+                spectra(lent_vis, row, lent_waves)
+                stage_one(1, first_ref[:, :own_width], halves_of(waves[buddy]))
+                pass_copy(row).wait_recv()
+                for q in range(rates):
+                    if q != 1:
+                        rate = flip_bits(z, q)
+                        arrived = passed[row, (q ^ 1) - 1]
+                        blocks = halves_of(waves[rate]) + halves_of(lent_waves[rate])
+                        stage_one(q, first_ref[...], blocks + [arrived, arrived])
+                keep[0, row] = stage_two(0)
+                keep[1, row] = stage_two(1)
+                cross_out[row, 0] = stage_two(3).astype(bf16)
+                cross_out[row, 1] = stage_two(2).astype(bf16)
+                cross_copy(row).start()
+
+            @pl.when(row >= LAG)
+            def _():
+                late = row - LAG
+                cross_copy(late).wait_recv()
+                keep[1, late] = keep[1, late] + cross_in[late, 1].astype(f32)
+                back_copy(late).start()
+                finish(late, keep[0, late] + cross_in[late, 0].astype(f32))
+
+            return carry
+
+        lax.fori_loop(0, count + LAG, one, 0)
+        for slot in range(1, n_tm):
+            lent_copy(slot, 0, count).wait_send()
+        cross_copy(0, count).wait_send()
+        back_copy(0, count).wait_send()
+
+    for slot in range(1, n_tm):
+        tm_copy(slot, 0, count).wait_send()
+
+
+def fringe_lending(n_tm, n_chan, pairs, tones, pcal_phase, samples):
+    _, periods, taken, _, stations, width = samples.shape
+    depth = width // INNER
+    lent = min(LENT, depth // 2)
+    rowed = samples.reshape(periods, taken, 2, stations // SUB, SUB, width // LANES, LANES)
+    rowed = rowed.transpose(0, 1, 2, 3, 5, 4, 6).reshape(periods, taken, 2, -1, LANES)
+    rates = periods * n_tm
+    count = pairs.shape[1] // n_tm
+    constants = lending_tables(n_chan, depth, lent)
+    firsts, twist_cos, _, last = constants
+    outer = twist_cos.shape[0]
+    lanes = last.shape[1] // 2
+    scale = 1.0 / (100.0 * taken * rates * n_chan * width)
+    tile = (outer, lanes)
+    dma = pltpu.SemaphoreType.DMA
+    kept = {
+        "codes": pltpu.VMEM((periods, taken, 2, width // LANES * stations, LANES), jnp.int32),
+        "x": pltpu.VMEM((periods, taken, 2, stations, depth, INNER), bf16),
+        "lent_x": pltpu.VMEM((periods, taken, 2, stations, lent, INNER), bf16),
+        "tones": pltpu.VMEM(tones.shape, jnp.int32),
+        "lent_tones": pltpu.VMEM(tones.shape, jnp.int32),
+        "pcal": pltpu.VMEM(pcal_phase.shape[1:], f32),
+        "cos": pltpu.VMEM((stations, depth, INNER), f32),
+        "sin": pltpu.VMEM((stations, depth, INNER), f32),
+        "lent_cos": pltpu.VMEM((stations, lent, INNER), f32),
+        "lent_sin": pltpu.VMEM((stations, lent, INNER), f32),
+        "first": pltpu.VMEM(firsts.shape[1:], bf16),
+        "tcos": pltpu.VMEM(twist_cos.shape, f32),
+        "tsin": pltpu.VMEM(twist_cos.shape, f32),
+        "last": pltpu.VMEM(last.shape, bf16),
+        "vis": pltpu.VMEM((n_tm, count, periods, 2 * depth, INNER), bf16),
+        "outbox": pltpu.VMEM((n_tm - 1, count, periods, 2 * depth, INNER), bf16),
+        "lent_vis": pltpu.VMEM((n_tm, count, periods, 2 * lent, INNER), bf16),
+        "lent_box": pltpu.VMEM((n_tm - 1, count, periods, 2 * lent, INNER), bf16),
+        "waves": pltpu.VMEM((rates, 2 * depth, INNER), f32),
+        "lent_waves": pltpu.VMEM((rates, 2 * lent, INNER), f32),
+        "passed": pltpu.VMEM((count, rates - 1, 2 * (depth - lent), INNER), bf16),
+        "twisted": pltpu.VMEM((rates * outer, 2 * INNER), bf16),
+        "keep": pltpu.VMEM((2, count) + tile, f32),
+        "cross_out": pltpu.VMEM((count, 2) + tile, bf16),
+        "cross_in": pltpu.VMEM((count, 2) + tile, bf16),
+        "phase_sem": dma((2,)),
+        "code_sem": dma((periods,)),
+        "table_sem": dma((len(constants),)),
+        "lend_send": dma((periods + 1,)),
+        "lend_recv": dma((periods + 1,)),
+        "tm_send": dma((n_tm - 1,)),
+        "tm_recv": dma((n_tm - 1, count)),
+        "tm_lent_send": dma((n_tm - 1,)),
+        "tm_lent_recv": dma((n_tm - 1, count)),
+        "pass_send": dma,
+        "pass_recv": dma((count,)),
+        "cross_send": dma,
+        "back_send": dma,
+        "sum_recv": dma((count,)),
+    }
+    given = ["pairs", "samples", "tones_in", "pcal_in", "firsts", "tcos_in", "tsin_in", "last_in"]
+    vmem = pl.BlockSpec(memory_space=pltpu.VMEM)
+    stay = pl.BlockSpec(memory_space=pltpu.HBM)
+    return pl.pallas_call(
+        functools.partial(lending_kernel, n_tm, scale, given + ["out"] + list(kept)),
+        out_shape=pltpu.VMEM((count, lanes // 2, outer), f32),
+        in_specs=[pl.BlockSpec(memory_space=pltpu.SMEM)] + [stay] * 7,
+        out_specs=vmem,
+        scratch_shapes=list(kept.values()),
+        compiler_params=pltpu.CompilerParams(
+            collective_id=0, has_side_effects=True, vmem_limit_bytes=57 << 20
+        ),
+        name="fringe_lending",
+    )(pairs, rowed, tones, pcal_phase, *(jnp.asarray(c) for c in constants))
+
+
 def shards(samples, pcal_phase, tone_index, baseline_pairs):
-    power = fringe(
+    n_chan = lax.axis_size("chan")
+    search = fringe_lending if n_chan == 4 else fringe
+    power = search(
         lax.axis_size("tm"),
-        lax.axis_size("chan"),
+        n_chan,
         baseline_pairs.T,
         tone_index.reshape(-1, LANES),
         pcal_phase,

time: 150 us -> 141 us (0.940)
  Pallas kernels: 148 us -> 140 us
    pallas_call x1, Pallas kernels: 148 us -> 140 us  [fringe_lending(): pl.pallas_call(functools.partial(lending_kernel, n_tm, scale, given + ['o...]
where the time goes in v2:
time: 141 us
  Pallas kernels  140 us (99%)
    pallas_call x1, Pallas kernels, fringe_lending(): pl.pallas_call(functools.partial(lending_kernel, n_tm, scale, given + ['o...  140 us

profile of v2, /device:TPU:0, one launch (start us, length us, event | category | flops | bytes accessed | tf_op | source)
XLA Modules:
  0.0 141.2 jit_solution(10672423057404595167)
XLA Ops:
  0.0 140.0 %fringe_lending.1 = f32[60,64,128]{2,1,0:T(8,128)S(1)} custom-call(s32[2,120]{1,0:T(2,128)} %bitcast.11, s32[2,4,2,1024,128]{4,3,2,1,0:T(8,128)} %bitcast.9, s32[64,128]{1,0:T(8,128)} %bitcast.10, f32[1,16,128]{2,1,0:T(8,128)} %flat_3_.1, bf16[4,256,336]{2,1,0:T(8,128)(2,1)} %constant.8.clone.flat_4_, f32[128,256]{1,0:T(8,128)} %constant.9.clone.flat_5_, ...), custom_call_target="tpu_custom_call" | custom-call | tf_op jit(solution)/shard_map/fringe_lending/pallas_call | solution.py:860
  140.0 1.3 copy.12

commit v3 on v2

--- a/solution.py
+++ b/solution.py
@@ -16,10 +16,11 @@
 INNER = 256
 GROUP = 1
 AHEAD = 2
-LAG = 3
+LAG = 4
 LENT = 8
-FAR_AHEAD = 16
-LENT_AHEAD = 10
+FAR_AHEAD = 18
+LENT_AHEAD = 13
+EARLY = 1
 
 two_pi = 2.0 * math.pi
 f32, bf16 = jnp.float32, jnp.bfloat16
@@ -415,7 +416,8 @@
     out_ref, codes, x_ref, lent_x = ref["out"], ref["codes"], ref["x"], ref["lent_x"]
     vis, outbox, lent_vis, lent_box = ref["vis"], ref["outbox"], ref["lent_vis"], ref["lent_box"]
     waves, lent_waves, passed = ref["waves"], ref["lent_waves"], ref["passed"]
-    twisted, keep, cross_out, cross_in = ref["twisted"], ref["keep"], ref["cross_out"], ref["cross_in"]
+    twisted, keep, home_out = ref["twisted"], ref["keep"], ref["home_out"]
+    cross_out, sums_in = ref["cross_out"], ref["sums_in"]
     first_ref, tcos_ref, tsin_ref, last_ref = ref["first"], ref["tcos"], ref["tsin"], ref["last"]
     pairs, tones = ref["pairs"], ref["tones"]
 
@@ -430,7 +432,7 @@
     me = lax.axis_index("tm")
     z = lax.axis_index("chan")
     buddy = flip_bits(z, 1)
-    across = flip_bits(z, 3)
+    across, far = flip_bits(z, 3), flip_bits(z, 2)
     is_end = lax.rem(z, 3) == 0
     is_inner = lax.rem(z, 3) != 0
 
@@ -468,7 +470,8 @@
         pl.semaphore_signal(
             barrier, inc=1, device_id={"tm": lax.rem(me + slot, n_tm)}, device_id_type=MESH
         )
-    pl.semaphore_signal(barrier, inc=1, device_id={"chan": buddy}, device_id_type=MESH)
+    for other in (buddy, far):
+        pl.semaphore_signal(barrier, inc=1, device_id={"chan": other}, device_id_type=MESH)
 
     @pl.when(is_inner)
     def _():
@@ -536,19 +539,16 @@
 
             @pl.when(is_end)
             def _():
-                pl.semaphore_wait(barrier, n_tm)
+                pl.semaphore_wait(barrier, n_tm + 1)
+                lend_tones.start()
 
             @pl.when(is_inner)
             def _():
-                pl.semaphore_wait(barrier, n_tm + 1)
+                pl.semaphore_wait(barrier, n_tm + 2)
 
         @pl.when(is_end)
         def _():
             lend(period).start()
-
-    @pl.when(is_end)
-    def _():
-        lend_tones.start()
 
     wait_all(constants)
 
@@ -585,27 +585,29 @@
             device_id_type=MESH,
         )
 
-    def cross_copy(row, size=1):
+    def sum_copy(index, row):
+        block = pl.ds(row, 1)
+        return pltpu.make_async_remote_copy(
+            src_ref=cross_out.at[index, block],
+            dst_ref=sums_in.at[0, block],
+            send_sem=ref["cross_send"],
+            recv_sem=ref["sum_recv"].at[row],
+            device_id={"chan": far if index else across},
+            device_id_type=MESH,
+        )
+
+    def home_copy(row, size=1):
         block = pl.ds(row, size)
         return pltpu.make_async_remote_copy(
-            src_ref=cross_out.at[block],
-            dst_ref=cross_in.at[block],
-            send_sem=ref["cross_send"],
-            recv_sem=ref["sum_recv"].at[row],
-            device_id={"chan": across},
-            device_id_type=MESH,
-        )
-
-    def back_copy(row, size=1):
-        block = pl.ds(row, size)
-        return pltpu.make_async_remote_copy(
-            src_ref=keep.at[1, block],
-            dst_ref=keep.at[1, block],
-            send_sem=ref["back_send"],
-            recv_sem=ref["sum_recv"].at[row],
+            src_ref=home_out.at[block],
+            dst_ref=sums_in.at[1, block],
+            send_sem=ref["home_send"],
+            recv_sem=ref["pass_recv"].at[row],
             device_id={"chan": buddy},
             device_id_type=MESH,
         )
+
+    cross_drain = pltpu.make_async_copy(cross_out, cross_out, ref["cross_send"])
 
     def correlate(slot, row, voltage, cos_ref, sin_ref, target, index):
         place = lax.rem(me + slot, n_tm) * count + row
@@ -700,9 +702,6 @@
             return carry
 
         lax.fori_loop(0, count, send_rows, 0)
-        for period in range(periods):
-            lend(period).wait_send()
-        lend_tones.wait_send()
 
         def one(row, carry):
             own_visibility(0, row)
@@ -715,14 +714,19 @@
                 passed[row, q - 1] = rest.astype(bf16)
             pass_copy(row).start()
             stage_one(0, first_ref[:, :own_width], halves_of(waves[z]))
-            keep[0, row] = stage_two(0)
-            return carry
-
-        lax.fori_loop(0, count, one, 0)
+            keep[row] = stage_two(0)
+            return carry
+
+        lax.fori_loop(0, min(EARLY, count), one, 0)
+        lend_tones.wait_send()
+        for period in range(periods):
+            lend(period).wait_send()
+        lax.fori_loop(min(EARLY, count), count, one, 0)
 
         def close(row, carry):
-            back_copy(row).wait_recv()
-            finish(row, keep[0, row] + keep[1, row])
+            home_copy(row).wait_recv()
+            sum_copy(1, row).wait_recv()
+            finish(row, keep[row] + sums_in[0, row].astype(f32) + sums_in[1, row].astype(f32))
             return carry
 
         lax.fori_loop(0, count, close, 0)
@@ -735,10 +739,10 @@
             return carry
 
         lax.fori_loop(0, min(FAR_AHEAD, count), send_rows, 0)
+        lend_tones.wait_recv()
+        station_tables(ref["lent_tones"], ref["lent_cos"], ref["lent_sin"])
         for period in range(periods):
             lend(period).wait_recv()
-        lend_tones.wait_recv()
-        station_tables(ref["lent_tones"], ref["lent_cos"], ref["lent_sin"])
 
         def lend_rows(row, carry):
             lent_outgoing(row)
@@ -761,8 +765,9 @@
                 lent_visibility(0, row)
                 for slot in range(1, n_tm):
                     tm_copy(slot, row).wait_recv()
+                spectra(vis, row, waves)
+                for slot in range(1, n_tm):
                     lent_copy(slot, row).wait_recv()
-                spectra(vis, row, waves)
                 spectra(lent_vis, row, lent_waves)
                 stage_one(1, first_ref[:, :own_width], halves_of(waves[buddy]))
                 pass_copy(row).wait_recv()
@@ -772,27 +777,27 @@
                         arrived = passed[row, (q ^ 1) - 1]
                         blocks = halves_of(waves[rate]) + halves_of(lent_waves[rate])
                         stage_one(q, first_ref[...], blocks + [arrived, arrived])
-                keep[0, row] = stage_two(0)
-                keep[1, row] = stage_two(1)
-                cross_out[row, 0] = stage_two(3).astype(bf16)
-                cross_out[row, 1] = stage_two(2).astype(bf16)
-                cross_copy(row).start()
+                keep[row] = stage_two(0)
+                home_out[row] = stage_two(1).astype(bf16)
+                cross_out[1, row] = stage_two(2).astype(bf16)
+                cross_out[0, row] = stage_two(3).astype(bf16)
+                sum_copy(1, row).start()
+                sum_copy(0, row).start()
+                home_copy(row).start()
 
             @pl.when(row >= LAG)
             def _():
                 late = row - LAG
-                cross_copy(late).wait_recv()
-                keep[1, late] = keep[1, late] + cross_in[late, 1].astype(f32)
-                back_copy(late).start()
-                finish(late, keep[0, late] + cross_in[late, 0].astype(f32))
+                sum_copy(0, late).wait_recv()
+                finish(late, keep[late] + sums_in[0, late].astype(f32))
 
             return carry
 
         lax.fori_loop(0, count + LAG, one, 0)
         for slot in range(1, n_tm):
             lent_copy(slot, 0, count).wait_send()
-        cross_copy(0, count).wait_send()
-        back_copy(0, count).wait_send()
+        cross_drain.wait()
+        home_copy(0, count).wait_send()
 
     for slot in range(1, n_tm):
         tm_copy(slot, 0, count).wait_send()
@@ -836,9 +841,10 @@
         "lent_waves": pltpu.VMEM((rates, 2 * lent, INNER), f32),
         "passed": pltpu.VMEM((count, rates - 1, 2 * (depth - lent), INNER), bf16),
         "twisted": pltpu.VMEM((rates * outer, 2 * INNER), bf16),
-        "keep": pltpu.VMEM((2, count) + tile, f32),
-        "cross_out": pltpu.VMEM((count, 2) + tile, bf16),
-        "cross_in": pltpu.VMEM((count, 2) + tile, bf16),
+        "keep": pltpu.VMEM((count,) + tile, f32),
+        "home_out": pltpu.VMEM((count,) + tile, bf16),
+        "cross_out": pltpu.VMEM((2, count) + tile, bf16),
+        "sums_in": pltpu.VMEM((2, count) + tile, bf16),
         "phase_sem": dma((2,)),
         "code_sem": dma((periods,)),
         "table_sem": dma((len(constants),)),
@@ -851,7 +857,7 @@
         "pass_send": dma,
         "pass_recv": dma((count,)),
         "cross_send": dma,
-        "back_send": dma,
+        "home_send": dma,
         "sum_recv": dma((count,)),
     }
     given = ["pairs", "samples", "tones_in", "pcal_in", "firsts", "tcos_in", "tsin_in", "last_in"]

time: 141 us -> 138 us (0.979)
  Pallas kernels: 140 us -> 137 us
    pallas_call x1, Pallas kernels: 140 us -> 137 us  [fringe_lending(): pl.pallas_call(functools.partial(lending_kernel, n_tm, scale, given + ['o...]
where the time goes in v3:
time: 138 us
  Pallas kernels  137 us (99%)
    pallas_call x1, Pallas kernels, fringe_lending(): pl.pallas_call(functools.partial(lending_kernel, n_tm, scale, given + ['o...  137 us

profile of v3, /device:TPU:0, one launch (start us, length us, event | category | flops | bytes accessed | tf_op | source)
XLA Modules:
  0.0 137.9 jit_solution(9591520386763099626)
XLA Ops:
  0.0 136.6 %fringe_lending.1 = f32[60,64,128]{2,1,0:T(8,128)S(1)} custom-call(s32[2,120]{1,0:T(2,128)} %bitcast.11, s32[2,4,2,1024,128]{4,3,2,1,0:T(8,128)} %bitcast.9, s32[64,128]{1,0:T(8,128)} %bitcast.10, f32[1,16,128]{2,1,0:T(8,128)} %flat_3_.1, bf16[4,256,336]{2,1,0:T(8,128)(2,1)} %constant.8.clone.flat_4_, f32[128,256]{1,0:T(8,128)} %constant.9.clone.flat_5_, ...), custom_call_target="tpu_custom_call" | custom-call | tf_op jit(solution)/shard_map/fringe_lending/pallas_call | solution.py:866
  136.6 1.3 copy.12

commit v4 on v3

--- a/solution.py
+++ b/solution.py
@@ -19,7 +19,7 @@
 LAG = 4
 LENT = 8
 FAR_AHEAD = 18
-LENT_AHEAD = 13
+LENT_AHEAD = 14
 EARLY = 1
 
 two_pi = 2.0 * math.pi
@@ -424,6 +424,7 @@
     periods, samples, _, stations, depth, inner = x_ref.shape
     lent = lent_x.shape[4]
     count = vis.shape[1]
+    pair = 2 if count % 2 == 0 else 1
     rates = periods * n_tm
     outer = tcos_ref.shape[0]
     lanes = last_ref.shape[1] // 2
@@ -558,7 +559,7 @@
             src_ref=outbox.at[slot - 1, block],
             dst_ref=vis.at[slot, block],
             send_sem=ref["tm_send"].at[slot - 1],
-            recv_sem=ref["tm_recv"].at[slot - 1, row],
+            recv_sem=ref["tm_recv"].at[slot - 1, lax.div(row, pair)],
             device_id={"tm": lax.rem(me + slot, n_tm)},
             device_id_type=MESH,
         )
@@ -569,7 +570,7 @@
             src_ref=lent_box.at[slot - 1, block],
             dst_ref=lent_vis.at[slot, block],
             send_sem=ref["tm_lent_send"].at[slot - 1],
-            recv_sem=ref["tm_lent_recv"].at[slot - 1, row],
+            recv_sem=ref["tm_lent_recv"].at[slot - 1, lax.div(row, pair)],
             device_id={"tm": lax.rem(me + slot, n_tm)},
             device_id_type=MESH,
         )
@@ -643,12 +644,18 @@
     def outgoing(row):
         for slot in range(1, n_tm):
             own_visibility(slot, row)
-            tm_copy(slot, row).start()
+
+            @pl.when(lax.rem(row, pair) == pair - 1)
+            def _():
+                tm_copy(slot, row - (pair - 1), pair).start()
 
     def lent_outgoing(row):
         for slot in range(1, n_tm):
             lent_visibility(slot, row)
-            lent_copy(slot, row).start()
+
+            @pl.when(lax.rem(row, pair) == pair - 1)
+            def _():
+                lent_copy(slot, row - (pair - 1), pair).start()
 
     def spectra(source, row, target):
         tall = target.shape[1] // 2
@@ -705,8 +712,12 @@
 
         def one(row, carry):
             own_visibility(0, row)
-            for slot in range(1, n_tm):
-                tm_copy(slot, row).wait_recv()
+
+            @pl.when(lax.rem(row, pair) == 0)
+            def _():
+                for slot in range(1, n_tm):
+                    tm_copy(slot, row, pair).wait_recv()
+
             spectra(vis, row, waves)
             for q in range(1, rates):
                 value = waves[flip_bits(z, q)]
@@ -763,11 +774,19 @@
             def _():
                 own_visibility(0, row)
                 lent_visibility(0, row)
-                for slot in range(1, n_tm):
-                    tm_copy(slot, row).wait_recv()
+
+                @pl.when(lax.rem(row, pair) == 0)
+                def _():
+                    for slot in range(1, n_tm):
+                        tm_copy(slot, row, pair).wait_recv()
+
                 spectra(vis, row, waves)
-                for slot in range(1, n_tm):
-                    lent_copy(slot, row).wait_recv()
+
+                @pl.when(lax.rem(row, pair) == 0)
+                def _():
+                    for slot in range(1, n_tm):
+                        lent_copy(slot, row, pair).wait_recv()
+
                 spectra(lent_vis, row, lent_waves)
                 stage_one(1, first_ref[:, :own_width], halves_of(waves[buddy]))
                 pass_copy(row).wait_recv()
@@ -795,12 +814,12 @@
 
         lax.fori_loop(0, count + LAG, one, 0)
         for slot in range(1, n_tm):
-            lent_copy(slot, 0, count).wait_send()
+            lent_copy(slot, jnp.int32(0), count).wait_send()
         cross_drain.wait()
         home_copy(0, count).wait_send()
 
     for slot in range(1, n_tm):
-        tm_copy(slot, 0, count).wait_send()
+        tm_copy(slot, jnp.int32(0), count).wait_send()
 
 
 def fringe_lending(n_tm, n_chan, pairs, tones, pcal_phase, samples):
@@ -818,6 +837,7 @@
     scale = 1.0 / (100.0 * taken * rates * n_chan * width)
     tile = (outer, lanes)
     dma = pltpu.SemaphoreType.DMA
+    pairs_of = count // 2 if count % 2 == 0 else count
     kept = {
         "codes": pltpu.VMEM((periods, taken, 2, width // LANES * stations, LANES), jnp.int32),
         "x": pltpu.VMEM((periods, taken, 2, stations, depth, INNER), bf16),
@@ -851,9 +871,9 @@
         "lend_send": dma((periods + 1,)),
         "lend_recv": dma((periods + 1,)),
         "tm_send": dma((n_tm - 1,)),
-        "tm_recv": dma((n_tm - 1, count)),
+        "tm_recv": dma((n_tm - 1, pairs_of)),
         "tm_lent_send": dma((n_tm - 1,)),
-        "tm_lent_recv": dma((n_tm - 1, count)),
+        "tm_lent_recv": dma((n_tm - 1, pairs_of)),
         "pass_send": dma,
         "pass_recv": dma((count,)),
         "cross_send": dma,

time: 138 us -> 138 us (level)
  no operation moved by 1% of the time
where the time goes in v4:
time: 138 us; the launch traced here: 137 us
  Pallas kernels  136 us (99%)
    pallas_call x1, Pallas kernels, fringe_lending(): pl.pallas_call(functools.partial(lending_kernel, n_tm, scale, given + ['o...  136 us

profile of v4, /device:TPU:0, one launch (start us, length us, event | category | flops | bytes accessed | tf_op | source)
XLA Modules:
  0.0 137.4 jit_solution(1587433428840208969)
XLA Ops:
  0.0 136.1 %fringe_lending.1 = f32[60,64,128]{2,1,0:T(8,128)S(1)} custom-call(s32[2,120]{1,0:T(2,128)} %bitcast.11, s32[2,4,2,1024,128]{4,3,2,1,0:T(8,128)} %bitcast.9, s32[64,128]{1,0:T(8,128)} %bitcast.10, f32[1,16,128]{2,1,0:T(8,128)} %flat_3_.1, bf16[4,256,336]{2,1,0:T(8,128)(2,1)} %constant.8.clone.flat_4_, f32[128,256]{1,0:T(8,128)} %constant.9.clone.flat_5_, ...), custom_call_target="tpu_custom_call" | custom-call | tf_op jit(solution)/shard_map/fringe_lending/pallas_call | solution.py:886
  136.1 1.3 copy.12
